TPU v7x, 32 devices: a whole 2x2x4 slice. The times are simulated.
32 devices in a mesh: replica: 4 (over z), model: 2 (over core), unit: 4 (over y, x).
Axes of the slice: x: 2, y: 2, z: 4, core: 2. Of those that a mesh axis runs over, the one named last changes fastest.
Arguments:
- partial_query: float32 [16, 768, 768], P(('unit', 'replica'), None, 'model'), parts along dimension 0, may hold values from -0.875 to 0.875
- partial_key: float32 [16, 768, 768], P(('unit', 'replica'), None, 'model'), parts along dimension 0, may hold values from -0.875 to 0.875
- partial_value: float32 [16, 768, 768], P(('unit', 'replica'), None, 'model'), parts along dimension 0, may hold values from -0.875 to 0.875
- partial_mixed: float32 [16, 768, 768], P(('unit', 'replica'), 'model'), parts along dimension 0, may hold values from -0.875 to 0.875
- partial_norm: float32 [16, 768], P(('unit', 'replica')), parts along dimension 0, may hold values from -8 to 8
- partial_bias: float32 [16, 768], P(('unit', 'replica')), parts along dimension 0, may hold values from -8 to 8
- master_query: float32 [3072, 768], P(('unit', 'replica'), 'model'), parts along dimension 0, may hold values from -0.21875 to 0.21875
- master_key: float32 [3072, 768], P(('unit', 'replica'), 'model'), parts along dimension 0, may hold values from -0.21875 to 0.21875
- master_value: float32 [3072, 768], P(('unit', 'replica'), 'model'), parts along dimension 0, may hold values from -0.21875 to 0.21875
- master_mixed: float32 [3072, 768], P(('unit', 'model'), 'replica'), parts along dimension 0, may hold values from -0.21875 to 0.21875
- master_norm: float32 [3072], P(('unit', 'replica')), parts along dimension 0, may hold values from 0.25 to 1.75
- master_bias: float32 [3072], P(('unit', 'replica')), parts along dimension 0, may hold values from -3 to 3
- memory_query: float32 [3072, 768], P(('unit', 'replica'), 'model'), parts along dimension 0, may hold values from -1.75 to 1.75
- memory_key: float32 [3072, 768], P(('unit', 'replica'), 'model'), parts along dimension 0, may hold values from -1.75 to 1.75
- memory_value: float32 [3072, 768], P(('unit', 'replica'), 'model'), parts along dimension 0, may hold values from -1.75 to 1.75
- memory_mixed: float32 [3072, 768], P(('unit', 'model'), 'replica'), parts along dimension 0, may hold values from -1.75 to 1.75
- memory_norm: float32 [3072], P(('unit', 'replica')), parts along dimension 0, may hold values from -1.75 to 1.75
- memory_bias: float32 [3072], P(('unit', 'replica')), parts along dimension 0, may hold values from -1.75 to 1.75
Outputs:
- compute_query: bfloat16 [3072, 768], P('unit', 'model'), parts along dimension 0
- compute_key: bfloat16 [3072, 768], P('unit', 'model'), parts along dimension 0
- compute_value: bfloat16 [3072, 768], P('unit', 'model'), parts along dimension 0
- compute_mixed: bfloat16 [3072, 768], P(('unit', 'model')), parts along dimension 0
- compute_norm: bfloat16 [3072], P('unit'), parts along dimension 0
- compute_bias: bfloat16 [3072], P('unit'), parts along dimension 0
- stepped_query: float32 [3072, 768], P(('unit', 'replica'), 'model'), parts along dimension 0
- stepped_key: float32 [3072, 768], P(('unit', 'replica'), 'model'), parts along dimension 0
- stepped_value: float32 [3072, 768], P(('unit', 'replica'), 'model'), parts along dimension 0
- stepped_mixed: float32 [3072, 768], P(('unit', 'model'), 'replica'), parts along dimension 0
- stepped_norm: float32 [3072], P(('unit', 'replica')), parts along dimension 0
- stepped_bias: float32 [3072], P(('unit', 'replica')), parts along dimension 0
- state_new_query: float32 [3072, 768], P(('unit', 'replica'), 'model'), parts along dimension 0
- state_new_key: float32 [3072, 768], P(('unit', 'replica'), 'model'), parts along dimension 0
- state_new_value: float32 [3072, 768], P(('unit', 'replica'), 'model'), parts along dimension 0
- state_new_mixed: float32 [3072, 768], P(('unit', 'model'), 'replica'), parts along dimension 0
- state_new_norm: float32 [3072], P(('unit', 'replica')), parts along dimension 0
- state_new_bias: float32 [3072], P(('unit', 'replica')), parts along dimension 0
There are 4 independent parts, one for each index of `unit`. A program takes and returns all parts, laid end to end along the dimension named above; each array names one. Nothing has to cross between parts.
All inputs are finite; a program needn't handle non-finite values.
Results may differ from a plain program's by a relative error of at most 0.0075.
Values may be sent and summed in bfloat16 or wider, within the bound.
A program may use at most 64 MiB of HBM per device.

v0:
```python
import jax
import jax.numpy as jnp
from jax import lax
from jax.sharding import PartitionSpec as P

learn_rate = 0.1
hold_rate = 0.7


def on_device(
    partial_query,
    partial_key,
    partial_value,
    partial_mixed,
    partial_norm,
    partial_bias,
    master_query,
    master_key,
    master_value,
    master_mixed,
    master_norm,
    master_bias,
    memory_query,
    memory_key,
    memory_value,
    memory_mixed,
    memory_norm,
    memory_bias,
):
    mean_query, mean_key, mean_value, mean_mixed = (
        lax.psum_scatter(
            partial_query[0].astype(jnp.bfloat16), "replica", scatter_dimension=0, tiled=True
        ).astype(jnp.float32),
        lax.psum_scatter(
            partial_key[0].astype(jnp.bfloat16), "replica", scatter_dimension=0, tiled=True
        ).astype(jnp.float32),
        lax.psum_scatter(
            partial_value[0].astype(jnp.bfloat16), "replica", scatter_dimension=0, tiled=True
        ).astype(jnp.float32),
        lax.psum_scatter(
            partial_mixed[0].astype(jnp.bfloat16), "replica", scatter_dimension=1, tiled=True
        ).astype(jnp.float32),
    )
    whole_norm, whole_bias = lax.psum((partial_norm[0], partial_bias[0]), "replica")
    place = lax.axis_index("replica")
    mean_norm = lax.dynamic_slice_in_dim(
        whole_norm, place * master_norm.shape[0], master_norm.shape[0]
    )
    mean_bias = lax.dynamic_slice_in_dim(
        whole_bias, place * master_bias.shape[0], master_bias.shape[0]
    )
    mean_rate = lax.axis_size("replica") ** (-0.5)
    mean_query = mean_query * mean_rate
    mean_key = mean_key * mean_rate
    mean_value = mean_value * mean_rate
    mean_mixed = mean_mixed * mean_rate
    mean_norm = mean_norm * mean_rate
    mean_bias = mean_bias * mean_rate
    state_new_query = hold_rate * memory_query + mean_query
    stepped_query = master_query - learn_rate * state_new_query
    state_new_key = hold_rate * memory_key + mean_key
    stepped_key = master_key - learn_rate * state_new_key
    state_new_value = hold_rate * memory_value + mean_value
    stepped_value = master_value - learn_rate * state_new_value
    state_new_mixed = hold_rate * memory_mixed + mean_mixed
    stepped_mixed = master_mixed - learn_rate * state_new_mixed
    state_new_norm = hold_rate * memory_norm + mean_norm
    stepped_norm = master_norm - learn_rate * state_new_norm
    state_new_bias = hold_rate * memory_bias + mean_bias
    stepped_bias = master_bias - learn_rate * state_new_bias
    compute_query, compute_key, compute_value, compute_mixed, compute_norm, compute_bias = (
        lax.all_gather(stepped_query.astype(jnp.bfloat16), "replica", axis=0, tiled=True),
        lax.all_gather(stepped_key.astype(jnp.bfloat16), "replica", axis=0, tiled=True),
        lax.all_gather(stepped_value.astype(jnp.bfloat16), "replica", axis=0, tiled=True),
        lax.all_gather(stepped_mixed.astype(jnp.bfloat16), "replica", axis=1, tiled=True),
        lax.all_gather(stepped_norm.astype(jnp.bfloat16), "replica", axis=0, tiled=True),
        lax.all_gather(stepped_bias.astype(jnp.bfloat16), "replica", axis=0, tiled=True),
    )
    return (
        compute_query,
        compute_key,
        compute_value,
        compute_mixed,
        compute_norm,
        compute_bias,
        stepped_query,
        stepped_key,
        stepped_value,
        stepped_mixed,
        stepped_norm,
        stepped_bias,
        state_new_query,
        state_new_key,
        state_new_value,
        state_new_mixed,
        state_new_norm,
        state_new_bias,
    )


def solution(mesh):
    in_specs = (
        P(("unit", "replica"), None, "model"),
        P(("unit", "replica"), None, "model"),
        P(("unit", "replica"), None, "model"),
        P(("unit", "replica"), "model", None),
        P(("unit", "replica"), None),
        P(("unit", "replica"), None),
        P(("unit", "replica"), "model"),
        P(("unit", "replica"), "model"),
        P(("unit", "replica"), "model"),
        P(("unit", "model"), "replica"),
        P(("unit", "replica")),
        P(("unit", "replica")),
        P(("unit", "replica"), "model"),
        P(("unit", "replica"), "model"),
        P(("unit", "replica"), "model"),
        P(("unit", "model"), "replica"),
        P(("unit", "replica")),
        P(("unit", "replica")),
    )
    out_specs = (
        P("unit", "model"),
        P("unit", "model"),
        P("unit", "model"),
        P(("unit", "model"), None),
        P("unit"),
        P("unit"),
        P(("unit", "replica"), "model"),
        P(("unit", "replica"), "model"),
        P(("unit", "replica"), "model"),
        P(("unit", "model"), "replica"),
        P(("unit", "replica")),
        P(("unit", "replica")),
        P(("unit", "replica"), "model"),
        P(("unit", "replica"), "model"),
        P(("unit", "replica"), "model"),
        P(("unit", "model"), "replica"),
        P(("unit", "replica")),
        P(("unit", "replica")),
    )
    return jax.shard_map(
        on_device, mesh=mesh, in_specs=in_specs, out_specs=out_specs, check_vma=False
    )
```

profile of v0, /device:TPU:0, one launch (start us, length us, event | category | flops | bytes accessed | tf_op | source)
XLA Modules:
  0.0 145.9 jit_solution(3519412508542594567)
XLA Ops:
  7.2 0.0 reduce-scatter.5.cloned.1.call-start
  7.2 2.2 %convert_bitcast_fusion.3 = bf16[768,384]{1,0:T(8,128)(2,1)} fusion(f32[1,768,384]{2,1,0:T(8,128)} %param.18), kind=kLoop, calls=%fused_computation.3 | loop fusion | flops 294912 | bytes 1769472 | tf_op jit(solution)/shard_map/convert_element_type | solution.py:32
  9.5 0.0 reduce-scatter.5.cloned.1.call-update
  9.5 0.0 copy-start.1
  9.5 0.0 reduce-scatter.7.cloned.1.call-start
  9.6 0.9 convert_bitcast_fusion.2
  10.5 0.0 reduce-scatter.7.cloned.1.call-update
  10.5 0.0 copy-start.2
  10.5 0.0 reduce-scatter.9.cloned.1.call-start
  10.5 0.4 copy-done.1
  11.0 0.9 convert_bitcast_fusion.1
  11.9 0.0 reduce-scatter.9.cloned.1.call-update
  11.9 0.0 copy-start.11
  11.9 0.0 copy-start.12
  11.9 0.0 copy-start.17
  11.9 0.0 copy-start.13
  11.9 0.0 copy-start.14
  12.0 0.0 copy-start.15
  12.0 0.0 copy-start.16
  12.0 0.0 copy-start.3
  12.0 0.0 copy-start.4
  12.0 0.0 reduce-scatter.11.cloned.1.call-start
  12.1 0.0 copy-done.2
  12.1 1.1 copy.36
  13.1 0.0 reduce-scatter.11.cloned.1.call-update
  13.1 0.0 copy-start.5
  13.2 0.0 copy-start.6
  13.3 14.5 %all-reduce.2 = (f32[768]{0:T(1024)S(1)}, f32[768]{0:T(1024)S(1)}) all-reduce(f32[768]{0:T(1024)S(1)} %reduce, f32[768]{0:T(1024)S(1)} %reduce.1), channel_id=1, replica_groups=mesh['replica'=4,'model'=2,'unit'=4] {'replica'}, use_global_device_ids=true, to_apply=%region_4.0 | all-reduce | flops 1536 | bytes 12288 | tf_op jit(solution)/shard_map/psum | solution.py:44
  27.8 0.6 dynamic-slice
  29.1 0.7 fusion
  29.7 0.2 dynamic-update-slice
  29.9 0.2 dynamic-update-slice.1
  30.1 8.9 %all-reduce.3 = (bf16[768]{0:T(1024)(128)(2,1)}, bf16[768]{0:T(1024)(128)(2,1)}) all-reduce(bf16[768]{0:T(1024)(128)(2,1)S(1)} %dynamic-update-slice, bf16[768]{0:T(1024)(128)(2,1)S(1)} %dynamic-update-slice.1), channel_id=1, replica_groups=mesh['replica'=4,'model'=2,'unit'=4] {'replica'}, use_global_device_ids=true, to_apply=%add | all-reduce | flops 1536 | bytes 6144
  39.0 1.8 %fusion.5 = (bf16[192,384]{1,0:T(8,128)(2,1)S(1)}, f32[192,384]{1,0:T(8,128)}, f32[192,384]{1,0:T(8,128)}) fusion(f32[192,384]{1,0:T(8,128)S(1)} %copy-done.3, bf16[192,384]{1,0:T(8,128)(2,1)} %reduce-scatter.5.cloned.1.call-done, f32[192,384]{1,0:T(8,128)S(1)} %copy-done.4), kind=kLoop, calls=%fused_computation.21 | loop fusion | flops 516096 | bytes 1474560 | tf_op jit(solution)/shard_map/convert_element_type | solution.py:72
  40.8 21.7 %all_gather.18 = bf16[768,384]{1,0:T(8,128)(2,1)S(1)} all-gather(bf16[192,384]{1,0:T(8,128)(2,1)S(1)} %get-tuple-element.55), channel_id=1, replica_groups=mesh['replica'=4,'model'=2,'unit'=4] {'replica'}, dimensions={0}, use_global_device_ids=true | all-gather | bytes 737280 | tf_op jit(solution)/shard_map/all_gather | solution.py:72
  62.5 0.3 reduce-scatter.7.cloned.1.call-done
  62.8 1.8 %fusion.4 = (bf16[192,384]{1,0:T(8,128)(2,1)S(1)}, f32[192,384]{1,0:T(8,128)}, f32[192,384]{1,0:T(8,128)}) fusion(f32[192,384]{1,0:T(8,128)S(1)} %copy-done.5, bf16[192,384]{1,0:T(8,128)(2,1)} %reduce-scatter.7.cloned.1.call-done, f32[192,384]{1,0:T(8,128)S(1)} %copy-done.6), kind=kLoop, calls=%fused_computation.20 | loop fusion | flops 516096 | bytes 1474560 | tf_op jit(solution)/shard_map/convert_element_type | solution.py:73
  64.6 20.7 %all_gather.19 = bf16[768,384]{1,0:T(8,128)(2,1)S(1)} all-gather(bf16[192,384]{1,0:T(8,128)(2,1)S(1)} %get-tuple-element.52), channel_id=1, replica_groups=mesh['replica'=4,'model'=2,'unit'=4] {'replica'}, dimensions={0}, use_global_device_ids=true | all-gather | bytes 737280 | tf_op jit(solution)/shard_map/all_gather | solution.py:73
  85.3 5.4 %reduce-scatter.9.cloned.1.call-done = bf16[192,384]{1,0:T(8,128)(2,1)} async-done(((bf16[768,384]{1,0:T(8,128)(2,1)}), bf16[192,384]{1,0:T(8,128)(2,1)}) %reduce-scatter.9.cloned.1.call-update) | async-done | bytes 147472 | tf_op jit(solution)/shard_map/reduce_scatter | solution.py:37
  90.7 1.8 %fusion.3 = (bf16[192,384]{1,0:T(8,128)(2,1)S(1)}, f32[192,384]{1,0:T(8,128)}, f32[192,384]{1,0:T(8,128)}) fusion(f32[192,384]{1,0:T(8,128)S(1)} %copy-done.7, bf16[192,384]{1,0:T(8,128)(2,1)} %reduce-scatter.9.cloned.1.call-done, f32[192,384]{1,0:T(8,128)S(1)} %copy-done.8), kind=kLoop, calls=%fused_computation.19 | loop fusion | flops 516096 | bytes 1474560 | tf_op jit(solution)/shard_map/convert_element_type | solution.py:74
  92.5 20.2 %all_gather.20 = bf16[768,384]{1,0:T(8,128)(2,1)S(1)} all-gather(bf16[192,384]{1,0:T(8,128)(2,1)S(1)} %get-tuple-element.49), channel_id=1, replica_groups=mesh['replica'=4,'model'=2,'unit'=4] {'replica'}, dimensions={0}, use_global_device_ids=true | all-gather | bytes 737280 | tf_op jit(solution)/shard_map/all_gather | solution.py:74
  112.7 5.4 %reduce-scatter.11.cloned.1.call-done = bf16[384,192]{0,1:T(8,128)(2,1)} async-done(((bf16[384,768]{0,1:T(8,128)(2,1)}), bf16[384,192]{0,1:T(8,128)(2,1)}) %reduce-scatter.11.cloned.1.call-update) | async-done | bytes 147472 | tf_op jit(solution)/shard_map/reduce_scatter | solution.py:40
  118.0 1.8 %fusion.2 = (bf16[384,192]{0,1:T(8,128)(2,1)S(1)}, f32[384,192]{0,1:T(8,128)}, f32[384,192]{0,1:T(8,128)}) fusion(f32[384,192]{0,1:T(8,128)S(1)} %copy-done.9, bf16[384,192]{0,1:T(8,128)(2,1)} %reduce-scatter.11.cloned.1.call-done, f32[384,192]{0,1:T(8,128)S(1)} %copy-done.10), kind=kLoop, calls=%fused_computation.18 | loop fusion | flops 516096 | bytes 1474560 | tf_op jit(solution)/shard_map/convert_element_type | solution.py:75
  119.8 16.0 %all_gather.21 = bf16[384,768]{0,1:T(8,128)(2,1)S(1)} all-gather(bf16[384,192]{0,1:T(8,128)(2,1)S(1)} %get-tuple-element.46), channel_id=1, replica_groups=mesh['replica'=4,'model'=2,'unit'=4] {'replica'}, dimensions={1}, use_global_device_ids=true | all-gather | bytes 737280 | tf_op jit(solution)/shard_map/all_gather | solution.py:75
  135.8 1.1 copy.37
  136.9 0.8 copy.43
  137.7 0.8 copy.44
  138.5 0.8 copy.45
  (26 shorter events, 0.1 us)
Async XLA Ops:
  7.2 2.4 %copy-start = (f32[1,768,384]{2,1,0:T(8,128)S(1)}, f32[1,768,384]{2,1,0:T(8,128)}, u32[]{:S(2)}) copy-start(f32[1,768,384]{2,1,0:T(8,128)} %param.19) | copy-start | bytes 3538948
  7.2 31.8 %reduce-scatter.5.cloned.1.call-start = ((), (), s32[]{:S(2)}) async-start(), calls=%async_computation.4 | async-start | bytes 737280 | tf_op jit(solution)/shard_map/reduce_scatter | solution.py:31
  9.5 1.5 %copy-start.1 = (f32[1,768,384]{2,1,0:T(8,128)S(1)}, f32[1,768,384]{2,1,0:T(8,128)}, u32[]{:S(2)}) copy-start(f32[1,768,384]{2,1,0:T(8,128)} %param.20) | copy-start | bytes 3538948
  9.5 53.3 %reduce-scatter.7.cloned.1.call-start = ((), (), s32[]{:S(2)}) async-start(), calls=%async_computation.5 | async-start | bytes 737280 | tf_op jit(solution)/shard_map/reduce_scatter | solution.py:34
  10.5 1.6 %copy-start.2 = (f32[1,384,768]{2,1,0:T(8,128)S(1)}, f32[1,384,768]{2,1,0:T(8,128)}, u32[]{:S(2)}) copy-start(f32[1,384,768]{2,1,0:T(8,128)} %param.21) | copy-start | bytes 3538948
  10.5 80.2 %reduce-scatter.9.cloned.1.call-start = ((), (), s32[]{:S(2)}) async-start(), calls=%async_computation.6 | async-start | bytes 737280 | tf_op jit(solution)/shard_map/reduce_scatter | solution.py:37
  11.9 1.3 copy-start.11
  11.9 1.3 copy-start.12
  11.9 15.8 %copy-start.17 = (u32[32]{0:T(128)S(1)}, u32[32]{0:T(128)}, u32[]{:S(2)}) copy-start(u32[32]{0:T(128)} %constant.31) | copy-start | bytes 388
  11.9 17.1 %copy-start.13 = (f32[192]{0:T(256)S(1)}, f32[192]{0:T(256)}, u32[]{:S(2)}) copy-start(f32[192]{0:T(256)} %param.29) | copy-start | bytes 2308
  11.9 17.1 %copy-start.14 = (f32[192]{0:T(256)S(1)}, f32[192]{0:T(256)}, u32[]{:S(2)}) copy-start(f32[192]{0:T(256)} %param.35) | copy-start | bytes 2308
  12.0 17.1 %copy-start.15 = (f32[192]{0:T(256)S(1)}, f32[192]{0:T(256)}, u32[]{:S(2)}) copy-start(f32[192]{0:T(256)} %param.28) | copy-start | bytes 2308
  12.0 17.1 %copy-start.16 = (f32[192]{0:T(256)S(1)}, f32[192]{0:T(256)}, u32[]{:S(2)}) copy-start(f32[192]{0:T(256)} %param.34) | copy-start | bytes 2308
  12.0 27.1 %copy-start.3 = (f32[192,384]{1,0:T(8,128)S(1)}, f32[192,384]{1,0:T(8,128)}, u32[]{:S(2)}) copy-start(f32[192,384]{1,0:T(8,128)} %param.24) | copy-start | bytes 884740
  12.0 27.1 %copy-start.4 = (f32[192,384]{1,0:T(8,128)S(1)}, f32[192,384]{1,0:T(8,128)}, u32[]{:S(2)}) copy-start(f32[192,384]{1,0:T(8,128)} %param.30) | copy-start | bytes 884740
  12.0 106.0 %reduce-scatter.11.cloned.1.call-start = ((), (), s32[]{:S(2)}) async-start(), calls=%async_computation.7 | async-start | bytes 737280 | tf_op jit(solution)/shard_map/reduce_scatter | solution.py:40
  13.1 49.7 %copy-start.5 = (f32[192,384]{1,0:T(8,128)S(1)}, f32[192,384]{1,0:T(8,128)}, u32[]{:S(2)}) copy-start(f32[192,384]{1,0:T(8,128)} %param.25) | copy-start | bytes 884740
  13.2 49.7 %copy-start.6 = (f32[192,384]{1,0:T(8,128)S(1)}, f32[192,384]{1,0:T(8,128)}, u32[]{:S(2)}) copy-start(f32[192,384]{1,0:T(8,128)} %param.31) | copy-start | bytes 884740
  62.5 28.2 %copy-start.7 = (f32[192,384]{1,0:T(8,128)S(1)}, f32[192,384]{1,0:T(8,128)}, u32[]{:S(2)}) copy-start(f32[192,384]{1,0:T(8,128)} %param.26) | copy-start | bytes 884740
  62.5 28.2 %copy-start.8 = (f32[192,384]{1,0:T(8,128)S(1)}, f32[192,384]{1,0:T(8,128)}, u32[]{:S(2)}) copy-start(f32[192,384]{1,0:T(8,128)} %param.32) | copy-start | bytes 884740
  85.3 32.8 %copy-start.9 = (f32[384,192]{0,1:T(8,128)S(1)}, f32[384,192]{0,1:T(8,128)}, u32[]{:S(2)}) copy-start(f32[384,192]{0,1:T(8,128)} %param.27) | copy-start | bytes 884740
  85.3 32.8 %copy-start.10 = (f32[384,192]{0,1:T(8,128)S(1)}, f32[384,192]{0,1:T(8,128)}, u32[]{:S(2)}) copy-start(f32[384,192]{0,1:T(8,128)} %param.33) | copy-start | bytes 884740
Sparse Core Ops, SparseCore 0:
  10.9 25.0 reduce-scatter.4
  38.8 23.9 reduce-scatter.6
  65.7 25.0 reduce-scatter.8
  93.4 24.5 reduce-scatter.10
where the time goes:
time: 146 us
  blocking collectives  102 us (70%)
  between operations  14.7 us (10%)
  other arithmetic  11.9 us (8%)
  waiting for transfers between devices  11.1 us (8%)
  local copies, waits for them, and re-layouts  6.11 us (4%)
    all_gather x1, blocking collectives, on_device(): lax.all_gather(stepped_query.astype(jnp.bfloat16), 'replica', axis=0, til...  21.7 us
    all_gather x1, blocking collectives, on_device(): lax.all_gather(stepped_key.astype(jnp.bfloat16), 'replica', axis=0, tiled...  20.7 us
    all_gather x1, blocking collectives, on_device(): lax.all_gather(stepped_value.astype(jnp.bfloat16), 'replica', axis=0, til...  20.2 us
    all_gather x1, blocking collectives, on_device(): lax.all_gather(stepped_mixed.astype(jnp.bfloat16), 'replica', axis=1, til...  16 us
    psum x1, blocking collectives, on_device(): lax.psum((partial_norm[0], partial_bias[0]), 'replica')  14.5 us
    unnamed x1, blocking collectives  8.92 us
    unnamed x46, local copies, waits for them, and re-layouts  6.11 us
    reduce_scatter x1, waiting for transfers between devices, on_device(): lax.psum_scatter(partial_value[0].astype(jnp.bfloat16), 'replica', scatte...  5.44 us
  transfers between devices with their start and end apart: 4, of which 3 were waited for; matrix products, arithmetic and copies ran while one was open for 7% of the time, Pallas kernels for 0%

commit v1 on v0

--- a/solution.py
+++ b/solution.py
@@ -1,7 +1,15 @@
+import functools
+
 import jax
 import jax.numpy as jnp
 from jax import lax
+from jax.experimental import pallas as pl
+from jax.experimental.pallas import tpu as pltpu
 from jax.sharding import PartitionSpec as P
+
+MESH = pl.DeviceIdType.MESH
+ORDER = (0, 3, 1, 2)
+TURNED = 1
 
 learn_rate = 0.1
 hold_rate = 0.7
@@ -98,6 +106,265 @@
     )
 
 
+def exchange(n, cuts, *refs):
+    vec_ref, part_refs, master_refs, memory_refs = refs[0], refs[1:5], refs[5:9], refs[9:13]
+    vecs_ref, comp_refs, stepped_refs, state_refs = refs[13], refs[14:18], refs[18:22], refs[22:26]
+    parts, masters, memories = refs[26:30], refs[30:34], refs[34:38]
+    stage, landed, gathered = refs[38:41]
+    load_sem, store_sem, vec_send, vec_recv, rs_send, rs_recv, ag_send, ag_recv = refs[41:49]
+
+    me = lax.axis_index("replica")
+    rate = n ** (-0.5)
+    rows = stage.shape[2]
+    span = rows * cuts
+    values = [gathered if k == TURNED else comp_refs[k] for k in range(4)]
+    steps = 4 * cuts
+
+    loads = []
+    for k in range(4):
+        loads.append(pltpu.make_async_copy(part_refs[k], parts[k], load_sem.at[k]))
+    for k in range(4):
+        loads.append(pltpu.make_async_copy(memory_refs[k], memories[k], load_sem.at[4 + k]))
+        loads.append(pltpu.make_async_copy(master_refs[k], masters[k], load_sem.at[8 + k]))
+    for load in loads:
+        load.start()
+    stores = [pltpu.make_async_copy(memories[k], state_refs[k], store_sem.at[k]) for k in range(4)]
+    stores += [pltpu.make_async_copy(masters[k], stepped_refs[k], store_sem.at[4 + k]) for k in range(4)]
+
+    barrier = pltpu.get_barrier_semaphore()
+    for k in range(1, n):
+        pl.semaphore_signal(
+            barrier, inc=1, device_id={"replica": lax.rem(me + k, n)}, device_id_type=MESH
+        )
+
+    def prepare(k):
+        loads[k].wait()
+        whole = parts[k][...].T if k == TURNED else parts[k][...]
+        for d in range(n):
+            for h in range(cuts):
+                at = d * span + h * rows
+                stage[k * cuts + h, d] = whole[at : at + rows, :].astype(stage.dtype)
+
+    right = lax.rem(me + 1, n)
+    left = lax.rem(me + n - 1, n)
+
+    def sum_copy(way, t, d):
+        return pltpu.make_async_remote_copy(
+            src_ref=stage.at[t, d],
+            dst_ref=landed.at[way, t, d],
+            send_sem=rs_send.at[t, d],
+            recv_sem=rs_recv.at[way, t, d],
+            device_id={"replica": right if way == 0 else left},
+            device_id_type=MESH,
+        )
+
+    def gather_copy(way, t, s):
+        k, h = divmod(t, cuts)
+        held = values[k].at[pl.ds(pl.multiple_of(s * span + h * rows, 16), rows), :]
+        return pltpu.make_async_remote_copy(
+            src_ref=held,
+            dst_ref=held,
+            send_sem=ag_send.at[way, t, s],
+            recv_sem=ag_recv.at[t, s],
+            device_id={"replica": right if way == 0 else left},
+            device_id_type=MESH,
+        )
+
+    def raw(t):
+        @pl.when(me == 0)
+        def _():
+            for d in range(n - 1, 0, -1):
+                sum_copy(0, t, d).start()
+
+        @pl.when(me == n - 1)
+        def _():
+            for d in range(n - 1):
+                sum_copy(1, t, d).start()
+
+    def relay(way, t, d):
+        sum_copy(way, t, d).wait_recv()
+        stage[t, d] = (
+            stage[t, d].astype(jnp.float32) + landed[way, t, d].astype(jnp.float32)
+        ).astype(stage.dtype)
+        sum_copy(way, t, d).start()
+
+    def relays(t):
+        for k in range(n - 1):
+            far = n - 1 - k
+            pl.when((me > 0) & (me < far))(functools.partial(relay, 0, t, far))
+            pl.when((me < n - 1) & (me > k))(functools.partial(relay, 1, t, k))
+
+    def finish(t):
+        k, h = divmod(t, cuts)
+        if h == 0:
+            loads[4 + 2 * k].wait()
+            loads[5 + 2 * k].wait()
+
+        def add(way):
+            sum_copy(way, t, me).wait_recv()
+            return landed[way, t, me].astype(jnp.float32)
+
+        def update(*ways):
+            total = stage[t, me].astype(jnp.float32)
+            for way in ways:
+                total = total + add(way)
+            mean = total * rate
+            at = slice(h * rows, (h + 1) * rows)
+            state = hold_rate * memories[k][at, :] + mean
+            memories[k][at, :] = state
+            stepped = masters[k][at, :] - learn_rate * state
+            masters[k][at, :] = stepped
+            values[k][pl.ds(pl.multiple_of(me * span + h * rows, 16), rows), :] = stepped.astype(stage.dtype)
+
+        @pl.when(me == 0)
+        def _():
+            update(1)
+            gather_copy(0, t, me).start()
+
+        @pl.when(me == n - 1)
+        def _():
+            update(0)
+            gather_copy(1, t, me).start()
+
+        @pl.when((me > 0) & (me < n - 1))
+        def _():
+            update(0, 1)
+            gather_copy(0, t, me).start()
+            gather_copy(1, t, me).start()
+
+        if h == cuts - 1:
+            stores[k].start()
+            stores[4 + k].start()
+
+    def pass_on(way, t, s):
+        gather_copy(way, t, s).wait_recv()
+        pl.when((me < n - 1) if way == 0 else (me > 0))(lambda: gather_copy(way, t, s).start())
+
+    def spread(t):
+        for k in range(1, n):
+            pl.when(me - k >= 0)(lambda: pass_on(0, t, me - k))
+            pl.when(me + k <= n - 1)(lambda: pass_on(1, t, me + k))
+        k, h = divmod(t, cuts)
+        if k == TURNED and h == cuts - 1:
+            comp_refs[k][...] = gathered[...].astype(jnp.float32).T.astype(stage.dtype)
+
+    def vec_copy(k):
+        return pltpu.make_async_remote_copy(
+            src_ref=vec_ref,
+            dst_ref=vecs_ref.at[me],
+            send_sem=vec_send.at[k],
+            recv_sem=vec_recv.at[k],
+            device_id={"replica": lax.rem(me + k, n)},
+            device_id_type=MESH,
+        )
+
+    prepare(0)
+    pl.semaphore_wait(barrier, n - 1)
+    for h in range(min(2, steps)):
+        if h % cuts == 0 and h > 0:
+            prepare(h // cuts)
+        raw(h)
+    for k in range(1, n):
+        vec_copy(k).start()
+    vecs_ref[me] = vec_ref[...]
+    for t in range(steps + 1):
+        ahead = t + 2
+        if ahead < steps:
+            if ahead % cuts == 0:
+                prepare(ahead // cuts)
+            raw(ahead)
+        if t < steps:
+            relays(t)
+            finish(t)
+        if t >= 1:
+            spread(t - 1)
+
+    for store in stores:
+        store.wait()
+    for k in range(1, n):
+        vec_copy(k).wait()
+    for t in range(steps):
+        for d in range(n):
+            pl.when(me < d)(lambda: sum_copy(0, t, d).wait_send())
+            pl.when(me > d)(lambda: sum_copy(1, t, d).wait_send())
+            pl.when((me >= d) & (me < n - 1))(lambda: gather_copy(0, t, d).wait_send())
+            pl.when((me <= d) & (me > 0))(lambda: gather_copy(1, t, d).wait_send())
+
+
+def line_on_device(n, *args):
+    grads, masters, memories = args[:6], args[6:12], args[12:18]
+    span, inner = masters[0].shape
+    cuts = 2 if span % 32 == 0 else 1
+    rows = span // cuts
+    wide, small = jnp.bfloat16, jnp.float32
+    vec = jnp.concatenate([grads[4][0], grads[5][0], masters[4], masters[5], memories[4], memories[5]])
+    vec = vec.reshape(-1, 128)
+    parts = [grads[k][0] for k in ORDER]
+    held = [[m[k].T if k == 3 else m[k] for k in ORDER] for m in (masters, memories)]
+    room = sum(p.size * 2 for p in parts) + n * (vec.size + 8 * 128) * 4 + 2**18
+    steps = 4 * cuts
+    hbm = pl.BlockSpec(memory_space=pltpu.HBM)
+    vmem = pl.BlockSpec(memory_space=pltpu.VMEM)
+    out_shape = (
+        [pltpu.VMEM((n, *vec.shape), small)]
+        + [pltpu.VMEM(p.shape, wide) for p in parts]
+        + [jax.ShapeDtypeStruct(m.shape, small) for m in held[0]] * 2
+    )
+    out = pl.pallas_call(
+        functools.partial(exchange, n, cuts),
+        out_shape=out_shape,
+        in_specs=[vmem] + [hbm] * 12,
+        out_specs=[vmem] * 5 + [hbm] * 8,
+        scratch_shapes=[pltpu.VMEM(p.shape, small) for p in parts]
+        + [pltpu.VMEM(m.shape, small) for m in held[0]] * 2
+        + [
+            pltpu.VMEM((steps, n, rows, inner), wide),
+            pltpu.VMEM((2, steps, n, rows, inner), wide),
+            pltpu.VMEM((n * span, inner), wide),
+            pltpu.SemaphoreType.DMA((12,)),
+            pltpu.SemaphoreType.DMA((8,)),
+            pltpu.SemaphoreType.DMA((n,)),
+            pltpu.SemaphoreType.DMA((n,)),
+            pltpu.SemaphoreType.DMA((steps, n)),
+            pltpu.SemaphoreType.DMA((2, steps, n)),
+            pltpu.SemaphoreType.DMA((2, steps, n)),
+            pltpu.SemaphoreType.DMA((steps, n)),
+        ],
+        compiler_params=pltpu.CompilerParams(
+            collective_id=0, has_side_effects=True, vmem_limit_bytes=67_043_328 - room
+        ),
+    )(vec, *parts, *held[0], *held[1])
+    vecs = out[0].reshape(n, -1)
+    whole = grads[4].shape[1]
+    place = lax.axis_index("replica") * masters[4].shape[0]
+    comp, stepped, state = (
+        [out[first + ORDER.index(k)] for k in range(4)] for first in (1, 5, 9)
+    )
+    stepped[3], state[3] = stepped[3].T, state[3].T
+    for k in range(2):
+        mean = jnp.sum(vecs[:, k * whole : (k + 1) * whole], axis=0) * (n ** (-0.5))
+        at = 2 * whole + k * masters[4].shape[0]
+        master = vecs[:, at : at + masters[4].shape[0]].reshape(-1)
+        at = at + 2 * masters[4].shape[0]
+        memory = vecs[:, at : at + masters[4].shape[0]].reshape(-1)
+        state_all = hold_rate * memory + mean
+        stepped_all = master - learn_rate * state_all
+        comp.append(stepped_all.astype(wide))
+        stepped.append(lax.dynamic_slice_in_dim(stepped_all, place, masters[4].shape[0]))
+        state.append(lax.dynamic_slice_in_dim(state_all, place, masters[4].shape[0]))
+    return (*comp, *stepped, *state)
+
+
+def chosen(n, *args):
+    span, inner = args[6].shape
+    height, width = args[9].shape
+    fits = n > 1 and span % 16 == 0 and width == span and height == inner
+    fits = fits and inner % 128 == 0 and (2 * args[4].shape[1] + 4 * args[10].shape[0]) % 128 == 0
+    if fits:
+        return line_on_device(n, *args)
+    return on_device(*args)
+
+
 def solution(mesh):
     in_specs = (
         P(("unit", "replica"), None, "model"),
@@ -140,5 +407,5 @@
         P(("unit", "replica")),
     )
     return jax.shard_map(
-        on_device, mesh=mesh, in_specs=in_specs, out_specs=out_specs, check_vma=False
-    )
+        functools.partial(chosen, mesh.shape["replica"]), mesh=mesh, in_specs=in_specs, out_specs=out_specs, check_vma=False
+    )

time: 146 us -> 149 us (1.021)
  Pallas kernels: 0 us -> 132 us
  blocking collectives: 102 us -> 0 us
  between operations: 14.7 us -> 0.7 us
  waiting for transfers between devices: 11.1 us -> 0 us
  other arithmetic: 11.9 us -> 2.08 us
  local copies, waits for them, and re-layouts: 6.11 us -> 13.3 us
    pallas_call x0 -> x1, Pallas kernels: none -> 132 us  [line_on_device(): pl.pallas_call(functools.partial(exchange, n, cuts), out_shape=out_shape,...]
    all_gather x4 -> x0, blocking collectives: 78.5 us -> none  [the longest x1 21.7 us: on_device(): lax.all_gather(stepped_query.astype(jnp.bfloat16), 'replica', axis=0, til...]
    psum x1 -> x0, blocking collectives: 14.5 us -> none  [on_device(): lax.psum((partial_norm[0], partial_bias[0]), 'replica')]
    convert_element_type x8 -> x1, other arithmetic: 11.8 us -> 0.59 us  [line_on_device(): comp.append(stepped_all.astype(wide))]
    reduce_scatter x4 -> x0, waiting for transfers between devices: 11.1 us -> none  [the longest x1 5.44 us: on_device(): lax.psum_scatter(partial_value[0].astype(jnp.bfloat16), 'replica', scatte...]
    unnamed x1 -> x0, blocking collectives: 8.92 us -> none
    unnamed x46 -> x29, local copies, waits for them, and re-layouts: 6.11 us -> 9.01 us
    dynamic_slice x0 -> x4, local copies, waits for them, and re-layouts: none -> 2.53 us  [the longest x2 1.27 us: line_on_device(): lax.dynamic_slice_in_dim(stepped_all, place, masters[4].shape[0])]
  transfers between devices with their start and end apart: 4 -> 0, of which waited for: 3 -> 0; matrix products, arithmetic and copies ran while one was open for 7% -> 0% of each run, Pallas kernels for 0% -> 0%
where the time goes in v1:
time: 149 us; the launch traced here: 148 us
  Pallas kernels  132 us (89%)
  local copies, waits for them, and re-layouts  13.3 us (9%)
  other arithmetic  2.08 us (1%)
    pallas_call x1, Pallas kernels, line_on_device(): pl.pallas_call(functools.partial(exchange, n, cuts), out_shape=out_shape,...  132 us
    unnamed x29, local copies, waits for them, and re-layouts  9.01 us

profile of v1, /device:TPU:0, one launch (start us, length us, event | category | flops | bytes accessed | tf_op | source)
XLA Modules:
  0.0 148.5 jit_solution(14483145223309922547)
XLA Ops:
  0.7 0.7 reduce
  1.4 0.7 reduce.1
  2.1 1.4 concatenate.3
  3.5 132.4 %shard_map.313 = (f32[4,18,128]{2,1,0:T(8,128)S(1)}, bf16[768,384]{1,0:T(8,128)(2,1)S(1)}, bf16[384,768]{1,0:T(8,128)(2,1)S(1)}, bf16[768,384]{1,0:T(8,128)(2,1)...) custom-call(f32[18,128]{1,0:T(8,128)} %bitcast.24, ...), custom_call_target="tpu_custom_call" | custom-call | tf_op jit(solution)/shard_map/pallas_call | solution.py:313
  135.9 0.1 slice_multiply_fusion
  136.0 0.1 mul.28
  136.1 0.1 mul.32
  136.2 0.1 reshape.56
  136.2 0.1 reshape.57
  136.3 0.6 fusion
  136.9 0.6 dynamic_slice.12
  137.6 0.6 dynamic_slice.13
  138.2 0.6 dynamic_slice.14
  138.8 0.6 dynamic_slice.15
  139.5 0.8 copy.51
  140.3 0.8 copy.52
  141.1 0.0 copy-start.7
  141.1 0.8 copy.53
  141.9 0.0 copy-start.6
  141.9 0.0 copy-start.5
  141.9 0.8 copy.54
  142.7 0.0 copy-start.4
  142.7 0.0 copy-done.7
  142.7 0.0 copy-start.3
  142.7 0.7 copy.55
  143.4 0.0 copy-done.6
  143.5 0.0 copy-start.2
  143.5 0.7 copy.56
  144.2 0.0 copy-done.5
  144.2 0.0 copy-start.1
  144.2 0.7 copy.57
  144.9 0.0 copy-done.4
  144.9 0.0 copy-start
  144.9 0.7 copy.58
  145.6 0.0 copy-done.3
  145.6 0.7 copy.59
  146.3 0.0 copy-done.2
  146.3 0.7 copy.60
  147.0 0.0 copy-done.1
  147.0 0.7 copy.61
  147.8 0.0 copy-done
  147.8 0.7 copy.62
  (2 shorter events, 0.0 us)
Async XLA Ops:
  141.1 1.6 %copy-start.7 = (f32[192,384]{1,0:T(8,128)S(1)}, f32[192,384]{1,0:T(8,128)}, u32[]{:S(2)}) copy-start(f32[192,384]{1,0:T(8,128)} %get-tuple-element.101) | copy-start | bytes 884740
  141.9 1.5 %copy-start.6 = (f32[192,384]{1,0:T(8,128)S(1)}, f32[192,384]{1,0:T(8,128)}, u32[]{:S(2)}) copy-start(f32[192,384]{1,0:T(8,128)} %get-tuple-element.102) | copy-start | bytes 884740
  141.9 2.3 %copy-start.5 = (f32[192,384]{1,0:T(8,128)S(1)}, f32[192,384]{1,0:T(8,128)}, u32[]{:S(2)}) copy-start(f32[192,384]{1,0:T(8,128)} %get-tuple-element.103) | copy-start | bytes 884740
  142.7 2.2 %copy-start.4 = (f32[192,384]{1,0:T(8,128)S(1)}, f32[192,384]{1,0:T(8,128)}, u32[]{:S(2)}) copy-start(f32[192,384]{1,0:T(8,128)} %get-tuple-element.39) | copy-start | bytes 884740
  142.7 2.9 %copy-start.3 = (f32[192,384]{1,0:T(8,128)S(1)}, f32[192,384]{1,0:T(8,128)}, u32[]{:S(2)}) copy-start(f32[192,384]{1,0:T(8,128)} %get-tuple-element.107) | copy-start | bytes 884740
  143.5 2.9 %copy-start.2 = (f32[192,384]{1,0:T(8,128)S(1)}, f32[192,384]{1,0:T(8,128)}, u32[]{:S(2)}) copy-start(f32[192,384]{1,0:T(8,128)} %get-tuple-element.108) | copy-start | bytes 884740
  144.2 2.9 %copy-start.1 = (f32[192,384]{1,0:T(8,128)S(1)}, f32[192,384]{1,0:T(8,128)}, u32[]{:S(2)}) copy-start(f32[192,384]{1,0:T(8,128)} %get-tuple-element.109) | copy-start | bytes 884740
  144.9 2.9 %copy-start = (f32[192,384]{1,0:T(8,128)S(1)}, f32[192,384]{1,0:T(8,128)}, u32[]{:S(2)}) copy-start(f32[192,384]{1,0:T(8,128)} %get-tuple-element.43) | copy-start | bytes 884740

commit v2 on v1

--- a/solution.py
+++ b/solution.py
@@ -294,7 +294,7 @@
 def line_on_device(n, *args):
     grads, masters, memories = args[:6], args[6:12], args[12:18]
     span, inner = masters[0].shape
-    cuts = 2 if span % 32 == 0 else 1
+    cuts = 1
     rows = span // cuts
     wide, small = jnp.bfloat16, jnp.float32
     vec = jnp.concatenate([grads[4][0], grads[5][0], masters[4], masters[5], memories[4], memories[5]])

time: 149 us -> 111 us (0.74)
  Pallas kernels: 132 us -> 94.2 us
    pallas_call x1, Pallas kernels: 132 us -> 94.2 us  [line_on_device(): pl.pallas_call(functools.partial(exchange, n, cuts), out_shape=out_shape,...]
where the time goes in v2:
time: 111 us; the launch traced here: 110 us
  Pallas kernels  94.2 us (85%)
  local copies, waits for them, and re-layouts  13.3 us (12%)
  other arithmetic  2.08 us (2%)
    pallas_call x1, Pallas kernels, line_on_device(): pl.pallas_call(functools.partial(exchange, n, cuts), out_shape=out_shape,...  94.2 us
    unnamed x29, local copies, waits for them, and re-layouts  9.01 us

profile of v2, /device:TPU:0, one launch (start us, length us, event | category | flops | bytes accessed | tf_op | source)
XLA Modules:
  0.0 110.2 jit_solution(13227202164117801173)
XLA Ops:
  0.7 0.7 reduce
  1.4 0.7 reduce.1
  2.1 1.4 %concatenate.3 = f32[2304]{0:T(1024)} concatenate(f32[768]{0:T(1024)S(1)} %reduce, f32[768]{0:T(1024)S(1)} %reduce.1, f32[192]{0:T(256)} %param.28, f32[192]{0:T(256)} %param.29, f32[192]{0:T(256)} %param.34, f32[192]{0:T(256)} %param.35), dimensions={0} | concatenate | bytes 18432 | tf_op jit(solution)/shard_map/concatenate | solution.py:300
  3.5 94.2 %shard_map.313 = (f32[4,18,128]{2,1,0:T(8,128)S(1)}, bf16[768,384]{1,0:T(8,128)(2,1)S(1)}, bf16[384,768]{1,0:T(8,128)(2,1)S(1)}, bf16[768,384]{1,0:T(8,128)(2,1)...) custom-call(f32[18,128]{1,0:T(8,128)} %bitcast.24, ...), custom_call_target="tpu_custom_call" | custom-call | tf_op jit(solution)/shard_map/pallas_call | solution.py:313
  97.7 0.1 slice_multiply_fusion
  97.7 0.1 mul.28
  97.8 0.1 mul.32
  97.9 0.1 reshape.56
  98.0 0.1 reshape.57
  98.1 0.6 fusion
  98.7 0.6 dynamic_slice.12
  99.3 0.6 dynamic_slice.13
  99.9 0.6 dynamic_slice.14
  100.6 0.6 dynamic_slice.15
  101.2 0.8 copy.51
  102.0 0.8 copy.52
  102.8 0.0 copy-start.7
  102.8 0.8 copy.53
  103.6 0.0 copy-start.6
  103.6 0.0 copy-start.5
  103.7 0.8 copy.54
  104.5 0.0 copy-start.4
  104.5 0.0 copy-done.7
  104.5 0.0 copy-start.3
  104.5 0.7 copy.55
  105.2 0.0 copy-done.6
  105.2 0.0 copy-start.2
  105.2 0.7 copy.56
  105.9 0.0 copy-done.5
  105.9 0.0 copy-start.1
  105.9 0.7 copy.57
  106.6 0.0 copy-done.4
  106.6 0.0 copy-start
  106.6 0.7 copy.58
  107.3 0.0 copy-done.3
  107.3 0.7 copy.59
  108.1 0.0 copy-done.2
  108.1 0.7 copy.60
  108.8 0.0 copy-done.1
  108.8 0.7 copy.61
  109.5 0.0 copy-done
  109.5 0.7 copy.62
  (2 shorter events, 0.0 us)
Async XLA Ops:
  102.8 1.6 %copy-start.7 = (f32[192,384]{1,0:T(8,128)S(1)}, f32[192,384]{1,0:T(8,128)}, u32[]{:S(2)}) copy-start(f32[192,384]{1,0:T(8,128)} %get-tuple-element.101) | copy-start | bytes 884740
  103.6 1.5 %copy-start.6 = (f32[192,384]{1,0:T(8,128)S(1)}, f32[192,384]{1,0:T(8,128)}, u32[]{:S(2)}) copy-start(f32[192,384]{1,0:T(8,128)} %get-tuple-element.102) | copy-start | bytes 884740
  103.6 2.3 %copy-start.5 = (f32[192,384]{1,0:T(8,128)S(1)}, f32[192,384]{1,0:T(8,128)}, u32[]{:S(2)}) copy-start(f32[192,384]{1,0:T(8,128)} %get-tuple-element.103) | copy-start | bytes 884740
  104.5 2.2 %copy-start.4 = (f32[192,384]{1,0:T(8,128)S(1)}, f32[192,384]{1,0:T(8,128)}, u32[]{:S(2)}) copy-start(f32[192,384]{1,0:T(8,128)} %get-tuple-element.39) | copy-start | bytes 884740
  104.5 2.9 %copy-start.3 = (f32[192,384]{1,0:T(8,128)S(1)}, f32[192,384]{1,0:T(8,128)}, u32[]{:S(2)}) copy-start(f32[192,384]{1,0:T(8,128)} %get-tuple-element.107) | copy-start | bytes 884740
  105.2 2.9 %copy-start.2 = (f32[192,384]{1,0:T(8,128)S(1)}, f32[192,384]{1,0:T(8,128)}, u32[]{:S(2)}) copy-start(f32[192,384]{1,0:T(8,128)} %get-tuple-element.108) | copy-start | bytes 884740
  105.9 2.9 %copy-start.1 = (f32[192,384]{1,0:T(8,128)S(1)}, f32[192,384]{1,0:T(8,128)}, u32[]{:S(2)}) copy-start(f32[192,384]{1,0:T(8,128)} %get-tuple-element.109) | copy-start | bytes 884740
  106.6 2.9 %copy-start = (f32[192,384]{1,0:T(8,128)S(1)}, f32[192,384]{1,0:T(8,128)}, u32[]{:S(2)}) copy-start(f32[192,384]{1,0:T(8,128)} %get-tuple-element.43) | copy-start | bytes 884740
